TPU v7x, 32 devices: a whole 2x2x4 slice. The times are simulated.
32 devices in a mesh: row: 4 (over y, x), col: 8 (over z, core).
Axes of the slice: x: 2, y: 2, z: 4, core: 2. Of those that a mesh axis runs over, the one named last changes fastest.
Arguments:
- pair_rep: bfloat16 [512, 512, 128], P('row', 'col'), may hold values from -6 to 6
- ln_gain: float32 [128], replicated, may hold values from 0.1 to 1.9
- ln_shift: float32 [128], replicated, may hold values from -3 to 3
- w_proj: bfloat16 [128, 512], replicated, may hold values from -0.5 to 0.5
- gate_bias: float32 [128], replicated, may hold values from -4 to 4
- w_bias: bfloat16 [128, 4], replicated, may hold values from -11 to 11
- w_out: bfloat16 [128, 128], replicated, may hold values from -0.5 to 0.5
- out_bias: float32 [128], replicated, may hold values from -3 to 3
- block_valid: int32 [4], replicated, may hold values from 0 to 1, as said below
Outputs:
- pair_out: bfloat16 [512, 512, 128], P('row', 'col')
Inputs may be any that keep to these rules, and one draw needn't show every extreme that they name: block_valid[b] is 1 when residues b * 128 to (b + 1) * 128 - 1 are present and 0 when they are padding; blocks 0 and 2 are always present, and at least one other block is always padding.
All inputs are finite; a program needn't handle non-finite values.
Results may differ from a plain program's by a relative error of at most 0.0082.
Values may be sent and summed in bfloat16 or wider, within the bound.
No kernel may reach another device: no remote copies, remote signals or barrier semaphores. Data moves between devices by JAX's collectives and lax.ppermute only.
A program may use at most 192 MiB of HBM per device.

v0:
```python
import math
import jax
import jax.numpy as jnp
from jax import lax
from jax.sharding import PartitionSpec as P

H = 4
HD = 32
BLK = 128


def layer_norm(values, ln_gain, ln_shift):
    widened = values.astype(jnp.float32)
    average = jnp.mean(widened, axis=-1, keepdims=True)
    spread = jnp.mean((widened - average) ** 2, axis=-1, keepdims=True)
    return ((widened - average) * lax.rsqrt(spread + 1e-05) * ln_gain + ln_shift).astype(
        jnp.bfloat16
    )


def residue_valid(block_valid, residues):
    blocks = block_valid.shape[0]
    block_width = residues // blocks
    owner = jnp.arange(residues, dtype=jnp.int32) // block_width
    matches = (owner[:, None] == jnp.arange(blocks, dtype=jnp.int32)[None, :]).astype(jnp.float32)
    return jnp.sum(matches * block_valid.astype(jnp.float32)[None, :], axis=1)


def start_state(width_j, query_count):
    running_max = jnp.full((H, width_j, query_count), -1e30, jnp.float32)
    denominator = jnp.zeros((H, width_j, query_count), jnp.float32)
    weighted = jnp.zeros((query_count, width_j, H, HD), jnp.float32)
    return (running_max, denominator, weighted)


def finish(carried):
    running_max, denominator, weighted = carried
    mixed = weighted / jnp.transpose(denominator, (2, 1, 0))[..., None]
    return mixed.reshape(mixed.shape[0], mixed.shape[1], H * HD).astype(jnp.bfloat16)


def fold_keys(carried, queries, key_rows, values, bias_part, validity):
    query_count, width_j, inner = queries.shape
    key_count = key_rows.shape[0]
    key_step = math.gcd(key_count, BLK)
    steps = key_count // key_step
    query_heads = queries.reshape(query_count, width_j, H, HD)
    key_blocks = key_rows.reshape(steps, key_step, width_j, H, HD)
    value_blocks = values.reshape(steps, key_step, width_j, H, HD)
    bias_blocks = jnp.transpose(bias_part.reshape(H, query_count, steps, key_step), (2, 0, 1, 3))
    mask_blocks = validity.reshape(steps, key_step)

    def update(carried_in, operands):
        key_part, value_part, bias_block, mask_part = operands
        running_max, denominator, weighted = carried_in
        scores = jnp.einsum(
            "ijhd,kjhd->hjik", query_heads, key_part, preferred_element_type=jnp.float32
        )
        scores = scores + bias_block[:, None, :, :]
        scores = jnp.where(mask_part[None, None, None, :] > 0, scores, jnp.float32(-1e30))
        renewed = jnp.maximum(running_max, jnp.max(scores, axis=-1))
        weights = jnp.exp(scores - renewed[..., None]) * mask_part[None, None, None, :]
        shrink = jnp.exp(running_max - renewed)
        denominator = denominator * shrink + jnp.sum(weights, axis=-1)
        product = jnp.einsum(
            "hjik,kjhd->ijhd",
            weights.astype(jnp.bfloat16),
            value_part,
            preferred_element_type=jnp.float32,
        )
        weighted = weighted * jnp.transpose(shrink, (2, 1, 0))[..., None] + product
        return (renewed, denominator, weighted)

    def scan_step(carried_in, operands):
        renewed = lax.cond(
            jnp.max(operands[3]) > 0, update, lambda kept, ignored: kept, carried_in, operands
        )
        return (renewed, None)

    result, ignored = lax.scan(
        scan_step, carried, (key_blocks, value_blocks, bias_blocks, mask_blocks)
    )
    return result


def shards(pair_rep, ln_gain, ln_shift, w_proj, gate_bias, w_bias, w_out, out_bias, block_valid):
    rows_dev, cols_dev, channels = pair_rep.shape
    row_count = lax.axis_size("row")
    row_id = lax.axis_index("row")
    col_id = lax.axis_index("col")
    residues = rows_dev * row_count
    inner = H * HD
    query_scale = HD ** (-0.5)
    validity = residue_valid(block_valid, residues)
    normed = layer_norm(pair_rep, ln_gain, ln_shift)
    flat_rows = normed.reshape(rows_dev * cols_dev, channels)
    bias_local = jnp.dot(flat_rows, w_bias, preferred_element_type=jnp.float32)
    bias_local = jnp.transpose(bias_local.reshape(rows_dev, cols_dev, H), (2, 1, 0))
    bias_cols = lax.all_gather(bias_local, "row", axis=2, tiled=True)
    regrouped = lax.all_to_all(normed, "row", split_axis=1, concat_axis=0, tiled=True)
    width_j = regrouped.shape[1]
    projected = jnp.dot(
        regrouped.reshape(residues * width_j, channels),
        w_proj[:, : 3 * inner],
        preferred_element_type=jnp.float32,
    )
    projected = projected.reshape(residues, width_j, 3 * inner)
    queries = (projected[..., :inner] * query_scale).astype(jnp.bfloat16)
    key_rows = projected[..., inner : 2 * inner].astype(jnp.bfloat16)
    values = projected[..., 2 * inner :].astype(jnp.bfloat16)
    bias_piece = lax.all_gather(bias_cols, "col", axis=1, tiled=True)
    span_rows = bias_piece.shape[1]
    query_block = math.gcd(span_rows, cols_dev)
    block_count = span_rows // query_block
    query_rows = queries
    query_rows = query_rows.reshape(block_count, query_block, width_j, inner)
    bias_blocks = jnp.transpose(
        bias_piece.reshape(H, block_count, query_block, residues), (1, 0, 2, 3)
    )

    def one_block(operands):
        query_part, bias_part = operands
        carried = fold_keys(
            start_state(width_j, query_block), query_part, key_rows, values, bias_part, validity
        )
        return finish(carried)

    results = lax.map(one_block, (query_rows, bias_blocks))
    gathered = results.reshape(span_rows, width_j, inner)
    attended = lax.all_to_all(gathered, "row", split_axis=0, concat_axis=1, tiled=True)
    gate_pre = jnp.dot(flat_rows, w_proj[:, 3 * inner :], preferred_element_type=jnp.float32)
    gate_pre = gate_pre.reshape(rows_dev, cols_dev, inner)
    gate_act = jax.nn.sigmoid(gate_pre + gate_bias)
    gated_rows = (gate_act * attended.astype(jnp.float32)).astype(jnp.bfloat16)
    update = jnp.dot(
        gated_rows.reshape(rows_dev * cols_dev, inner), w_out, preferred_element_type=jnp.float32
    )
    update = update.reshape(rows_dev, cols_dev, channels) + out_bias
    row_valid = lax.dynamic_slice_in_dim(validity, row_id * rows_dev, rows_dev, 0)
    col_valid = lax.dynamic_slice_in_dim(validity, col_id * cols_dev, cols_dev, 0)
    pair_mask = row_valid[:, None] * col_valid[None, :]
    return (pair_rep.astype(jnp.float32) + update * pair_mask[..., None]).astype(jnp.bfloat16)


def solution(mesh):
    return jax.shard_map(
        shards,
        mesh=mesh,
        in_specs=(P("row", "col", None), P(), P(), P(), P(), P(), P(), P(), P()),
        out_specs=P("row", "col", None),
        check_vma=False,
    )
```

profile of v0, /device:TPU:0, one launch (start us, length us, event | category | flops | bytes accessed | tf_op | source)
XLA Modules:
  0.0 358.7 jit_solution(1915389312735172597)
XLA Ops:
  6.6 3.5 convert_reduce_fusion
  10.1 6.1 %fusion.16 = f32[128,64]{0,1:T(8,128)S(1)} fusion(f32[128,64]{0,1:T(8,128)S(1)} %broadcast_multiply_fusion.1, bf16[128,64,128]{2,1,0:T(8,128)(2,1)S(1)} %copy-done.1), kind=kLoop, calls=%fused_computation.31 | loop fusion | flops 4186112 | bytes 2162688 | tf_op jit(solution)/shard_map/reduce_sum | solution.py:15
  16.3 5.0 %fusion.19 = bf16[128,64,128]{2,0,1:T(8,128)(2,1)S(1)} fusion(f32[128]{0:T(128)S(1)} %copy-done.7, f32[128]{0:T(128)S(1)} %copy-done.8, f32[128,64]{0,1:T(8,128)S(1)} %add_rsqrt_fusion, f32[128,64]{0,1:T(8,128)S(1)} %broadcast_multiply_fusion.1, bf16[128,64,128]{2,1,0:T(8,128)(2,1)S(1)} %copy-done.1), kind=kLoop, calls=%fused_computation.34 | loop fusion | flops 6291456 | bytes 4260864 | tf_op jit(solution)/shard_map/convert_element_type | solution.py:16
  23.2 12.3 %all_gather.6 = f32[4,64,512]{2,0,1:T(4,128)} all-gather(f32[4,64,128]{2,0,1:T(4,128)S(1)} %convolution_bitcast_fusion.1), channel_id=1, replica_groups=mesh['row'=4,'col'=8] {'row'}, dimensions={2}, use_global_device_ids=true | all-gather | bytes 655360 | tf_op jit(solution)/shard_map/all_gather | solution.py:99
  35.5 3.8 %all-to-all-start = ((bf16[128,64,128]{2,0,1:T(8,128)(2,1)}), bf16[128,64,128]{2,0,1:T(8,128)(2,1)S(1)}, u32[]{:S(2)}, u32[]{:S(2)}) async-start(bf16[128,64,128]{2,0,1:T(8,128)(2,1)} %copy-done.3), calls=%async_computation | async-start | bytes 4194304 | tf_op jit(solution)/shard_map/all_to_all | solution.py:100
  39.4 23.1 %all-to-all-done = bf16[128,64,128]{2,0,1:T(8,128)(2,1)S(1)} async-done(((bf16[128,64,128]{2,0,1:T(8,128)(2,1)}), bf16[128,64,128]{2,0,1:T(8,128)(2,1)S(1)}, u32[]{:S(2)}, u32[]{:S(2)}) %all-to-all-start) | async-done | bytes 2097184 | tf_op jit(solution)/shard_map/all_to_all | solution.py:100
  63.4 6.3 %fusion.38 = (bf16[512,16,384]{2,0,1:T(8,128)(2,1)S(1)}, f32[512,16,384]{2,0,1:T(8,128)}) fusion(bf16[512,16,128]{2,0,1:T(8,128)(2,1)S(1)} %bitcast.98, bf16[128,512]{1,0:T(8,128)(2,1)S(1)} %copy-done.5), kind=kOutput, calls=%fused_computation.65 | convolution fusion | flops 808452096 | bytes 21069824 | tf_op jit(solution)/shard_map/dot_general | solution.py:102
  69.7 3.2 fusion.37
  73.0 2.9 copy.79
  75.9 2.3 reshape.131
  78.1 3.9 %copy.80 = bf16[512,16,128]{0,2,1:T(8,128)(2,1)} copy(bf16[512,16,128]{2,0,1:T(8,128)(2,1)} %get-tuple-element.292) | data formatting | bytes 4194304 | tf_op jit(solution)/shard_map/while | solution.py:128
  82.0 4.0 %reshape.132 = bf16[4,128,16,4,32]{1,0,4,3,2:T(4,128)(2,1)} reshape(bf16[512,16,128]{0,2,1:T(8,128)(2,1)} %copy.80) | data formatting | bytes 4194304 | tf_op jit(solution)/shard_map/while/body/eval_jaxpr/reshape | solution.py:49
  86.0 4.2 %fusion.21 = bf16[512,16,128]{2,0,1:T(8,128)(2,1)} fusion(f32[512,16,384]{2,0,1:T(8,128)} %get-tuple-element.295), kind=kLoop, calls=%fused_computation.37 | loop fusion | flops 2097152 | bytes 6291456 | tf_op jit(solution)/shard_map/convert_element_type | solution.py:108
  90.2 5.4 %copy.101 = f32[4,8,64,512]{3,2,0,1:T(8,128)} copy(f32[4,8,64,512]{3,0,2,1:T(4,128)} %bitcast.100) | data formatting | bytes 8388608 | tf_op jit(solution)/shard_map/reshape | solution.py:118
  95.6 212.3 %while.27 = (s32[]{:T(128)}, bf16[8,64,16,128]{3,2,1,0:T(8,128)(2,1)}, bf16[512,16,128]{0,2,1:T(8,128)(2,1)}, bf16[512,16,128]{0,2,1:T(8,128)(2,1)}, f32[8,4,64,...) while((s32[]{:T(128)}, ...), condition=%wide.wide.region_11.12_spmd, body=%wide.wide.region_3.11_spmd.sunk | while | flops 72364288 | bytes 25006472 | solution.py:128
  98.2 3.3 copy.116
  101.6 3.5 copy.120
  105.2 15.8 %while.28 = (s32[]{:T(128)}, f32[4,16,64]{2,1,0:T(8,128)S(1)}, f32[4,16,64]{2,1,0:T(8,128)S(1)}, f32[64,16,4,32]{0,3,2,1:T(8,128)S(1)}, f32[4,128]{1,0:T(4,128)S...) while((s32[]{:T(128)}, f32[4,16,64]{2,1,0:T(8,128)S(1)}, ...), condition=%wide.region_10.10_spmd, body=%wide.region_4.9_spmd.sunk | while | flops 72102144 | bytes 9457287 | solution.py:80
  106.5 5.2 %conditional.2 = ((f32[4,16,64]{2,1,0:T(8,128)S(1)}, f32[4,16,64]{2,1,0:T(8,128)S(1)}, f32[64,16,4,32]{0,3,2,1:T(8,128)S(1)})) conditional(s32[]{:T(128)} %convert_element_type.97, (f32[4,16,64]{2,1,0:T(8,128)S(1)}, f32[4,16,64]{2,1,0:T(8,128)S(1)}, f32[64,16,4,32]{0,3,2,1:T(8,128)S(1)}) %tuple.69, (f32[1,128]{1,0:T(1,128)S(1)}, ...), branch_computations={%region_6.5_spmd, %region_7.8_spmd} | conditional | flops 72102016 | bytes 9456036 | solution.py:75
  114.4 5.2 %conditional.2 = ((f32[4,16,64]{2,1,0:T(8,128)S(1)}, f32[4,16,64]{2,1,0:T(8,128)S(1)}, f32[64,16,4,32]{0,3,2,1:T(8,128)S(1)})) conditional(s32[]{:T(128)} %convert_element_type.97, (f32[4,16,64]{2,1,0:T(8,128)S(1)}, f32[4,16,64]{2,1,0:T(8,128)S(1)}, f32[64,16,4,32]{0,3,2,1:T(8,128)S(1)}) %tuple.69, (f32[1,128]{1,0:T(1,128)S(1)}, ...), branch_computations={%region_6.5_spmd, %region_7.8_spmd} | conditional | flops 72102016 | bytes 9456036 | solution.py:75
  124.8 3.3 copy.116
  128.1 3.5 copy.120
  131.7 15.8 %while.28 = (s32[]{:T(128)}, f32[4,16,64]{2,1,0:T(8,128)S(1)}, f32[4,16,64]{2,1,0:T(8,128)S(1)}, f32[64,16,4,32]{0,3,2,1:T(8,128)S(1)}, f32[4,128]{1,0:T(4,128)S...) while((s32[]{:T(128)}, f32[4,16,64]{2,1,0:T(8,128)S(1)}, ...), condition=%wide.region_10.10_spmd, body=%wide.region_4.9_spmd.sunk | while | flops 72102144 | bytes 9457287 | solution.py:80
  133.1 5.2 %conditional.2 = ((f32[4,16,64]{2,1,0:T(8,128)S(1)}, f32[4,16,64]{2,1,0:T(8,128)S(1)}, f32[64,16,4,32]{0,3,2,1:T(8,128)S(1)})) conditional(s32[]{:T(128)} %convert_element_type.97, (f32[4,16,64]{2,1,0:T(8,128)S(1)}, f32[4,16,64]{2,1,0:T(8,128)S(1)}, f32[64,16,4,32]{0,3,2,1:T(8,128)S(1)}) %tuple.69, (f32[1,128]{1,0:T(1,128)S(1)}, ...), branch_computations={%region_6.5_spmd, %region_7.8_spmd} | conditional | flops 72102016 | bytes 9456036 | solution.py:75
  140.9 5.2 %conditional.2 = ((f32[4,16,64]{2,1,0:T(8,128)S(1)}, f32[4,16,64]{2,1,0:T(8,128)S(1)}, f32[64,16,4,32]{0,3,2,1:T(8,128)S(1)})) conditional(s32[]{:T(128)} %convert_element_type.97, (f32[4,16,64]{2,1,0:T(8,128)S(1)}, f32[4,16,64]{2,1,0:T(8,128)S(1)}, f32[64,16,4,32]{0,3,2,1:T(8,128)S(1)}) %tuple.69, (f32[1,128]{1,0:T(1,128)S(1)}, ...), branch_computations={%region_6.5_spmd, %region_7.8_spmd} | conditional | flops 72102016 | bytes 9456036 | solution.py:75
  141.0 2.0 fusion.1
  151.3 3.3 copy.116
  154.7 3.5 copy.120
  158.3 15.8 %while.28 = (s32[]{:T(128)}, f32[4,16,64]{2,1,0:T(8,128)S(1)}, f32[4,16,64]{2,1,0:T(8,128)S(1)}, f32[64,16,4,32]{0,3,2,1:T(8,128)S(1)}, f32[4,128]{1,0:T(4,128)S...) while((s32[]{:T(128)}, f32[4,16,64]{2,1,0:T(8,128)S(1)}, ...), condition=%wide.region_10.10_spmd, body=%wide.region_4.9_spmd.sunk | while | flops 72102144 | bytes 9457287 | solution.py:80
  159.6 5.2 %conditional.2 = ((f32[4,16,64]{2,1,0:T(8,128)S(1)}, f32[4,16,64]{2,1,0:T(8,128)S(1)}, f32[64,16,4,32]{0,3,2,1:T(8,128)S(1)})) conditional(s32[]{:T(128)} %convert_element_type.97, (f32[4,16,64]{2,1,0:T(8,128)S(1)}, f32[4,16,64]{2,1,0:T(8,128)S(1)}, f32[64,16,4,32]{0,3,2,1:T(8,128)S(1)}) %tuple.69, (f32[1,128]{1,0:T(1,128)S(1)}, ...), branch_computations={%region_6.5_spmd, %region_7.8_spmd} | conditional | flops 72102016 | bytes 9456036 | solution.py:75
  167.5 5.2 %conditional.2 = ((f32[4,16,64]{2,1,0:T(8,128)S(1)}, f32[4,16,64]{2,1,0:T(8,128)S(1)}, f32[64,16,4,32]{0,3,2,1:T(8,128)S(1)})) conditional(s32[]{:T(128)} %convert_element_type.97, (f32[4,16,64]{2,1,0:T(8,128)S(1)}, f32[4,16,64]{2,1,0:T(8,128)S(1)}, f32[64,16,4,32]{0,3,2,1:T(8,128)S(1)}) %tuple.69, (f32[1,128]{1,0:T(1,128)S(1)}, ...), branch_computations={%region_6.5_spmd, %region_7.8_spmd} | conditional | flops 72102016 | bytes 9456036 | solution.py:75
  177.9 3.3 copy.116
  181.2 3.5 copy.120
  184.8 15.8 %while.28 = (s32[]{:T(128)}, f32[4,16,64]{2,1,0:T(8,128)S(1)}, f32[4,16,64]{2,1,0:T(8,128)S(1)}, f32[64,16,4,32]{0,3,2,1:T(8,128)S(1)}, f32[4,128]{1,0:T(4,128)S...) while((s32[]{:T(128)}, f32[4,16,64]{2,1,0:T(8,128)S(1)}, ...), condition=%wide.region_10.10_spmd, body=%wide.region_4.9_spmd.sunk | while | flops 72102144 | bytes 9457287 | solution.py:80
  186.1 5.2 %conditional.2 = ((f32[4,16,64]{2,1,0:T(8,128)S(1)}, f32[4,16,64]{2,1,0:T(8,128)S(1)}, f32[64,16,4,32]{0,3,2,1:T(8,128)S(1)})) conditional(s32[]{:T(128)} %convert_element_type.97, (f32[4,16,64]{2,1,0:T(8,128)S(1)}, f32[4,16,64]{2,1,0:T(8,128)S(1)}, f32[64,16,4,32]{0,3,2,1:T(8,128)S(1)}) %tuple.69, (f32[1,128]{1,0:T(1,128)S(1)}, ...), branch_computations={%region_6.5_spmd, %region_7.8_spmd} | conditional | flops 72102016 | bytes 9456036 | solution.py:75
  194.0 5.2 %conditional.2 = ((f32[4,16,64]{2,1,0:T(8,128)S(1)}, f32[4,16,64]{2,1,0:T(8,128)S(1)}, f32[64,16,4,32]{0,3,2,1:T(8,128)S(1)})) conditional(s32[]{:T(128)} %convert_element_type.97, (f32[4,16,64]{2,1,0:T(8,128)S(1)}, f32[4,16,64]{2,1,0:T(8,128)S(1)}, f32[64,16,4,32]{0,3,2,1:T(8,128)S(1)}) %tuple.69, (f32[1,128]{1,0:T(1,128)S(1)}, ...), branch_computations={%region_6.5_spmd, %region_7.8_spmd} | conditional | flops 72102016 | bytes 9456036 | solution.py:75
  204.4 3.3 copy.116
  207.7 3.5 copy.120
  211.3 15.8 %while.28 = (s32[]{:T(128)}, f32[4,16,64]{2,1,0:T(8,128)S(1)}, f32[4,16,64]{2,1,0:T(8,128)S(1)}, f32[64,16,4,32]{0,3,2,1:T(8,128)S(1)}, f32[4,128]{1,0:T(4,128)S...) while((s32[]{:T(128)}, f32[4,16,64]{2,1,0:T(8,128)S(1)}, ...), condition=%wide.region_10.10_spmd, body=%wide.region_4.9_spmd.sunk | while | flops 72102144 | bytes 9457287 | solution.py:80
  212.7 5.2 %conditional.2 = ((f32[4,16,64]{2,1,0:T(8,128)S(1)}, f32[4,16,64]{2,1,0:T(8,128)S(1)}, f32[64,16,4,32]{0,3,2,1:T(8,128)S(1)})) conditional(s32[]{:T(128)} %convert_element_type.97, (f32[4,16,64]{2,1,0:T(8,128)S(1)}, f32[4,16,64]{2,1,0:T(8,128)S(1)}, f32[64,16,4,32]{0,3,2,1:T(8,128)S(1)}) %tuple.69, (f32[1,128]{1,0:T(1,128)S(1)}, ...), branch_computations={%region_6.5_spmd, %region_7.8_spmd} | conditional | flops 72102016 | bytes 9456036 | solution.py:75
  212.7 2.0 fusion.1
  220.6 5.2 %conditional.2 = ((f32[4,16,64]{2,1,0:T(8,128)S(1)}, f32[4,16,64]{2,1,0:T(8,128)S(1)}, f32[64,16,4,32]{0,3,2,1:T(8,128)S(1)})) conditional(s32[]{:T(128)} %convert_element_type.97, (f32[4,16,64]{2,1,0:T(8,128)S(1)}, f32[4,16,64]{2,1,0:T(8,128)S(1)}, f32[64,16,4,32]{0,3,2,1:T(8,128)S(1)}) %tuple.69, (f32[1,128]{1,0:T(1,128)S(1)}, ...), branch_computations={%region_6.5_spmd, %region_7.8_spmd} | conditional | flops 72102016 | bytes 9456036 | solution.py:75
  220.6 2.0 fusion.1
  230.9 3.3 copy.116
  234.3 3.5 copy.120
  237.9 15.8 %while.28 = (s32[]{:T(128)}, f32[4,16,64]{2,1,0:T(8,128)S(1)}, f32[4,16,64]{2,1,0:T(8,128)S(1)}, f32[64,16,4,32]{0,3,2,1:T(8,128)S(1)}, f32[4,128]{1,0:T(4,128)S...) while((s32[]{:T(128)}, f32[4,16,64]{2,1,0:T(8,128)S(1)}, ...), condition=%wide.region_10.10_spmd, body=%wide.region_4.9_spmd.sunk | while | flops 72102144 | bytes 9457287 | solution.py:80
  239.2 5.2 %conditional.2 = ((f32[4,16,64]{2,1,0:T(8,128)S(1)}, f32[4,16,64]{2,1,0:T(8,128)S(1)}, f32[64,16,4,32]{0,3,2,1:T(8,128)S(1)})) conditional(s32[]{:T(128)} %convert_element_type.97, (f32[4,16,64]{2,1,0:T(8,128)S(1)}, f32[4,16,64]{2,1,0:T(8,128)S(1)}, f32[64,16,4,32]{0,3,2,1:T(8,128)S(1)}) %tuple.69, (f32[1,128]{1,0:T(1,128)S(1)}, ...), branch_computations={%region_6.5_spmd, %region_7.8_spmd} | conditional | flops 72102016 | bytes 9456036 | solution.py:75
  239.3 2.0 fusion.1
  247.1 5.2 %conditional.2 = ((f32[4,16,64]{2,1,0:T(8,128)S(1)}, f32[4,16,64]{2,1,0:T(8,128)S(1)}, f32[64,16,4,32]{0,3,2,1:T(8,128)S(1)})) conditional(s32[]{:T(128)} %convert_element_type.97, (f32[4,16,64]{2,1,0:T(8,128)S(1)}, f32[4,16,64]{2,1,0:T(8,128)S(1)}, f32[64,16,4,32]{0,3,2,1:T(8,128)S(1)}) %tuple.69, (f32[1,128]{1,0:T(1,128)S(1)}, ...), branch_computations={%region_6.5_spmd, %region_7.8_spmd} | conditional | flops 72102016 | bytes 9456036 | solution.py:75
  257.5 3.3 copy.116
  260.8 3.5 copy.120
  264.4 15.8 %while.28 = (s32[]{:T(128)}, f32[4,16,64]{2,1,0:T(8,128)S(1)}, f32[4,16,64]{2,1,0:T(8,128)S(1)}, f32[64,16,4,32]{0,3,2,1:T(8,128)S(1)}, f32[4,128]{1,0:T(4,128)S...) while((s32[]{:T(128)}, f32[4,16,64]{2,1,0:T(8,128)S(1)}, ...), condition=%wide.region_10.10_spmd, body=%wide.region_4.9_spmd.sunk | while | flops 72102144 | bytes 9457287 | solution.py:80
  265.8 5.2 %conditional.2 = ((f32[4,16,64]{2,1,0:T(8,128)S(1)}, f32[4,16,64]{2,1,0:T(8,128)S(1)}, f32[64,16,4,32]{0,3,2,1:T(8,128)S(1)})) conditional(s32[]{:T(128)} %convert_element_type.97, (f32[4,16,64]{2,1,0:T(8,128)S(1)}, f32[4,16,64]{2,1,0:T(8,128)S(1)}, f32[64,16,4,32]{0,3,2,1:T(8,128)S(1)}) %tuple.69, (f32[1,128]{1,0:T(1,128)S(1)}, ...), branch_computations={%region_6.5_spmd, %region_7.8_spmd} | conditional | flops 72102016 | bytes 9456036 | solution.py:75
  273.6 5.2 %conditional.2 = ((f32[4,16,64]{2,1,0:T(8,128)S(1)}, f32[4,16,64]{2,1,0:T(8,128)S(1)}, f32[64,16,4,32]{0,3,2,1:T(8,128)S(1)})) conditional(s32[]{:T(128)} %convert_element_type.97, (f32[4,16,64]{2,1,0:T(8,128)S(1)}, f32[4,16,64]{2,1,0:T(8,128)S(1)}, f32[64,16,4,32]{0,3,2,1:T(8,128)S(1)}) %tuple.69, (f32[1,128]{1,0:T(1,128)S(1)}, ...), branch_computations={%region_6.5_spmd, %region_7.8_spmd} | conditional | flops 72102016 | bytes 9456036 | solution.py:75
  284.0 3.3 copy.116
  287.4 3.5 copy.120
  291.0 15.8 %while.28 = (s32[]{:T(128)}, f32[4,16,64]{2,1,0:T(8,128)S(1)}, f32[4,16,64]{2,1,0:T(8,128)S(1)}, f32[64,16,4,32]{0,3,2,1:T(8,128)S(1)}, f32[4,128]{1,0:T(4,128)S...) while((s32[]{:T(128)}, f32[4,16,64]{2,1,0:T(8,128)S(1)}, ...), condition=%wide.region_10.10_spmd, body=%wide.region_4.9_spmd.sunk | while | flops 72102144 | bytes 9457287 | solution.py:80
  292.3 5.2 %conditional.2 = ((f32[4,16,64]{2,1,0:T(8,128)S(1)}, f32[4,16,64]{2,1,0:T(8,128)S(1)}, f32[64,16,4,32]{0,3,2,1:T(8,128)S(1)})) conditional(s32[]{:T(128)} %convert_element_type.97, (f32[4,16,64]{2,1,0:T(8,128)S(1)}, f32[4,16,64]{2,1,0:T(8,128)S(1)}, f32[64,16,4,32]{0,3,2,1:T(8,128)S(1)}) %tuple.69, (f32[1,128]{1,0:T(1,128)S(1)}, ...), branch_computations={%region_6.5_spmd, %region_7.8_spmd} | conditional | flops 72102016 | bytes 9456036 | solution.py:75
  300.2 5.2 %conditional.2 = ((f32[4,16,64]{2,1,0:T(8,128)S(1)}, f32[4,16,64]{2,1,0:T(8,128)S(1)}, f32[64,16,4,32]{0,3,2,1:T(8,128)S(1)})) conditional(s32[]{:T(128)} %convert_element_type.97, (f32[4,16,64]{2,1,0:T(8,128)S(1)}, f32[4,16,64]{2,1,0:T(8,128)S(1)}, f32[64,16,4,32]{0,3,2,1:T(8,128)S(1)}) %tuple.69, (f32[1,128]{1,0:T(1,128)S(1)}, ...), branch_computations={%region_6.5_spmd, %region_7.8_spmd} | conditional | flops 72102016 | bytes 9456036 | solution.py:75
  307.9 3.8 %all-to-all-start.1 = ((bf16[512,16,128]{2,1,0:T(8,128)(2,1)}), bf16[512,16,128]{2,1,0:T(8,128)(2,1)S(1)}, u32[]{:S(2)}, u32[]{:S(2)}) async-start(bf16[512,16,128]{2,1,0:T(8,128)(2,1)} %bitcast.102), calls=%async_computation.1 | async-start | bytes 4194304 | tf_op jit(solution)/shard_map/all_to_all | solution.py:130
  312.0 24.0 %all-to-all-done.1 = bf16[512,16,128]{2,1,0:T(8,128)(2,1)S(1)} async-done(((bf16[512,16,128]{2,1,0:T(8,128)(2,1)}), bf16[512,16,128]{2,1,0:T(8,128)(2,1)S(1)}, u32[]{:S(2)}, u32[]{:S(2)}) %all-to-all-start.1) | async-done | bytes 2097184 | tf_op jit(solution)/shard_map/all_to_all | solution.py:130
  336.4 2.6 copy.83
  339.1 8.5 %fusion.20 = bf16[128,64,128]{2,0,1:T(8,128)(2,1)} fusion(f32[128,64]{0,1:T(8,128)S(1)} %broadcast_multiply_fusion, f32[128]{0:T(128)S(1)} %copy-done.10, bf16[128,64,128]{2,1,0:T(8,128)(2,1)S(1)} %copy-done.2, f32[128,64,128]{2,1,0:T(8,128)} %bitcast.101, bf16[128,64,128]{2,0,1:T(8,128)(2,1)} %copy-done.3, f32[128]{0:T(128)S(1)} %copy-done.11, ...), kind=kOutput, calls=%fused_computation.35 | convolution fusion | flops 548405248 | bytes 10585088 | tf_op jit(solution)/shard_map/dot_general | solution.py:135
  347.5 4.3 %copy.85 = bf16[128,64,128]{2,1,0:T(8,128)(2,1)} copy(bf16[128,64,128]{2,0,1:T(8,128)(2,1)} %fusion.20) | data formatting | bytes 4194304 | tf_op jit(solution)/shard_map/convert_element_type | solution.py:142
  (331 shorter events, 130.4 us)
Async XLA Ops:
  6.5 332.5 %copy-start = (bf16[128,128]{1,0:T(8,128)(2,1)S(1)}, bf16[128,128]{1,0:T(8,128)(2,1)}, u32[]{:S(2)}) copy-start(bf16[128,128]{1,0:T(8,128)(2,1)} %param.21) | copy-start | bytes 98308
  6.5 3.6 copy-start.1
  6.5 9.7 %copy-start.8 = (f32[128]{0:T(128)S(1)}, f32[128]{0:T(128)}, u32[]{:S(2)}) copy-start(f32[128]{0:T(128)} %param.16) | copy-start | bytes 1540
  6.5 9.7 %copy-start.7 = (f32[128]{0:T(128)S(1)}, f32[128]{0:T(128)}, u32[]{:S(2)}) copy-start(f32[128]{0:T(128)} %param.17) | copy-start | bytes 1540
  6.5 83.7 %all-gather.2.cloned.1.call-start = ((), (), s32[]{:S(2)}) async-start(), calls=%async_computation.2 | async-start | bytes 4718592 | tf_op jit(solution)/shard_map/all_gather | solution.py:111
  16.3 6.3 %copy-start.6 = (bf16[128,4]{0,1:T(4,128)(2,1)S(1)}, bf16[128,4]{0,1:T(4,128)(2,1)}, u32[]{:S(2)}) copy-start(bf16[128,4]{0,1:T(4,128)(2,1)} %param.20) | copy-start | bytes 3076
  21.2 1.3 copy-start.3
  35.5 3.8 %copy-start.9 = (s32[4]{0:T(128)S(1)}, s32[4]{0:T(128)}, u32[]{:S(2)}) copy-start(s32[4]{0:T(128)} %param.23) | copy-start | bytes 52
  35.5 27.0 %all-to-all-start = ((bf16[128,64,128]{2,0,1:T(8,128)(2,1)}), bf16[128,64,128]{2,0,1:T(8,128)(2,1)S(1)}, u32[]{:S(2)}, u32[]{:S(2)}) async-start(bf16[128,64,128]{2,0,1:T(8,128)(2,1)} %copy-done.3), calls=%async_computation | async-start | bytes 4194304 | tf_op jit(solution)/shard_map/all_to_all | solution.py:100
  62.5 0.9 copy-start.5
  75.8 2.3 copy-start.4
  307.9 28.1 %all-to-all-start.1 = ((bf16[512,16,128]{2,1,0:T(8,128)(2,1)}), bf16[512,16,128]{2,1,0:T(8,128)(2,1)S(1)}, u32[]{:S(2)}, u32[]{:S(2)}) async-start(bf16[512,16,128]{2,1,0:T(8,128)(2,1)} %bitcast.102), calls=%async_computation.1 | async-start | bytes 4194304 | tf_op jit(solution)/shard_map/all_to_all | solution.py:130
  336.4 2.6 copy-start.2
  336.4 2.6 copy-start.10
  336.4 2.6 copy-start.11
Sparse Core Ops, SparseCore 0:
  35.6 47.1 all-gather.1
where the time goes:
time: 362 us; the launch traced here: 359 us
  local copies, waits for them, and re-layouts  116 us (32%)
  matrix products  74.5 us (21%)
  other arithmetic  64.1 us (18%)
  waiting for transfers between devices  47.1 us (13%)
  loops' own time  23.6 us (7%)
  between operations  13.6 us (4%)
  blocking collectives  12.3 us (3%)
  starting transfers between devices  7.66 us (2%)
    while x32, local copies, waits for them, and re-layouts, fold_keys(): lax.scan(scan_step, carried, (key_blocks, value_blocks, bias_blocks, mask...  55.1 us
    dot_general x16, matrix products, update(): jnp.einsum('ijhd,kjhd->hjik', query_heads, key_part, preferred_element_ty...  31.4 us
    dot_general x16, matrix products, update(): jnp.einsum('hjik,kjhd->ijhd', weights.astype(jnp.bfloat16), value_part, p...  27.6 us
    all_to_all x1, waiting for transfers between devices, shards(): lax.all_to_all(gathered, 'row', split_axis=0, concat_axis=1, tiled=True)  24 us
    all_to_all x1, waiting for transfers between devices, shards(): lax.all_to_all(normed, 'row', split_axis=1, concat_axis=0, tiled=True)  23.1 us
    reduce_max x32, other arithmetic, scan_step(): jnp.max(operands[3]) > 0  21.5 us
    convert_element_type x16, other arithmetic, update(): weights.astype(jnp.bfloat16)  21.5 us
    another operation x8, loops' own time, fold_keys(): lax.scan(scan_step, carried, (key_blocks, value_blocks, bias_blocks, mask...  21.4 us
  transfers between devices with their start and end apart: 3, of which 2 were waited for; matrix products, arithmetic and copies ran while one was open for 8% of the time, Pallas kernels for 0%

commit v1 on v0

--- a/solution.py
+++ b/solution.py
@@ -7,6 +7,29 @@
 H = 4
 HD = 32
 BLK = 128
+
+
+def cut_along(array, dim, count):
+    lengths = array.shape
+    blocks = array.reshape(*lengths[:dim], count, lengths[dim] // count, *lengths[dim + 1 :])
+    return jnp.moveaxis(blocks, dim, 0)
+
+
+def laid_out(blocks, dim):
+    lengths = list(blocks.shape[1:])
+    lengths[dim] *= blocks.shape[0]
+    return jnp.moveaxis(blocks, 0, dim).reshape(lengths)
+
+
+def exchange_in_pairs(value, axis, split_dim, concat_dim):
+    length, here = (lax.axis_size(axis), lax.axis_index(axis))
+    blocks = cut_along(value, split_dim, length)
+    outs = [blocks[here]]
+    for lap in range(1, length):
+        sent = blocks[here ^ lap]
+        outs.append(lax.ppermute(sent, axis, [(i, i ^ lap) for i in range(length)]))
+    blocks = jnp.stack(outs)[here ^ jnp.arange(length)]
+    return laid_out(blocks, concat_dim)
 
 
 def layer_norm(values, ln_gain, ln_shift):
@@ -127,7 +150,7 @@
 
     results = lax.map(one_block, (query_rows, bias_blocks))
     gathered = results.reshape(span_rows, width_j, inner)
-    attended = lax.all_to_all(gathered, "row", split_axis=0, concat_axis=1, tiled=True)
+    attended = exchange_in_pairs(gathered, "row", 0, 1)
     gate_pre = jnp.dot(flat_rows, w_proj[:, 3 * inner :], preferred_element_type=jnp.float32)
     gate_pre = gate_pre.reshape(rows_dev, cols_dev, inner)
     gate_act = jax.nn.sigmoid(gate_pre + gate_bias)

time: 362 us -> 363 us (level)
    all_to_all x1 -> x0, waiting for transfers between devices: 24 us -> none  [shards(): lax.all_to_all(gathered, 'row', split_axis=0, concat_axis=1, tiled=True)]
    ppermute x0 -> x3, waiting for transfers between devices: none -> 20.6 us  [exchange_in_pairs(): outs.append(lax.ppermute(sent, axis, [(i, i ^ lap) for i in range(length)]))]
    all_to_all x1 -> x0, starting transfers between devices: 3.83 us -> none  [shards(): lax.all_to_all(gathered, 'row', split_axis=0, concat_axis=1, tiled=True)]
  transfers between devices with their start and end apart: 3 -> 5, of which waited for: 2 -> 3; matrix products, arithmetic and copies ran while one was open for 8% -> 7% of each run, Pallas kernels for 0% -> 0%
where the time goes in v1:
time: 363 us; the launch traced here: 359 us
  local copies, waits for them, and re-layouts  118 us (33%)
  matrix products  74.7 us (21%)
  other arithmetic  66.7 us (18%)
  waiting for transfers between devices  43.7 us (12%)
  loops' own time  23.5 us (6%)
  between operations  13.6 us (4%)
  blocking collectives  12.3 us (3%)
  starting transfers between devices  7.38 us (2%)
    while x32, local copies, waits for them, and re-layouts, fold_keys(): lax.scan(scan_step, carried, (key_blocks, value_blocks, bias_blocks, mask...  55.3 us
    dot_general x16, matrix products, update(): jnp.einsum('ijhd,kjhd->hjik', query_heads, key_part, preferred_element_ty...  31.4 us
    dot_general x16, matrix products, update(): jnp.einsum('hjik,kjhd->ijhd', weights.astype(jnp.bfloat16), value_part, p...  27.6 us
    all_to_all x1, waiting for transfers between devices, shards(): lax.all_to_all(normed, 'row', split_axis=1, concat_axis=0, tiled=True)  23 us
    convert_element_type x16, other arithmetic, update(): weights.astype(jnp.bfloat16)  21.5 us
    reduce_max x32, other arithmetic, scan_step(): jnp.max(operands[3]) > 0  21.4 us
    another operation x8, loops' own time, fold_keys(): lax.scan(scan_step, carried, (key_blocks, value_blocks, bias_blocks, mask...  21.3 us
    ppermute x3, waiting for transfers between devices, exchange_in_pairs(): outs.append(lax.ppermute(sent, axis, [(i, i ^ lap) for i in range(length)]))  20.6 us
  transfers between devices with their start and end apart: 5, of which 3 were waited for; matrix products, arithmetic and copies ran while one was open for 7% of the time, Pallas kernels for 0%

profile of v1, /device:TPU:0, one launch (start us, length us, event | category | flops | bytes accessed | tf_op | source)
XLA Modules:
  0.0 359.4 jit_solution(13729432276633699756)
XLA Ops:
  6.6 3.5 convert_reduce_fusion
  10.1 6.1 %fusion.16 = f32[128,64]{0,1:T(8,128)S(1)} fusion(f32[128,64]{0,1:T(8,128)S(1)} %broadcast_multiply_fusion.1, bf16[128,64,128]{2,1,0:T(8,128)(2,1)S(1)} %copy-done.1), kind=kLoop, calls=%fused_computation.32 | loop fusion | flops 4186112 | bytes 2162688 | tf_op jit(solution)/shard_map/reduce_sum | solution.py:38
  16.3 5.0 %fusion.19 = bf16[128,64,128]{2,0,1:T(8,128)(2,1)S(1)} fusion(f32[128]{0:T(128)S(1)} %copy-done.8, f32[128]{0:T(128)S(1)} %copy-done.9, f32[128,64]{0,1:T(8,128)S(1)} %add_rsqrt_fusion, f32[128,64]{0,1:T(8,128)S(1)} %broadcast_multiply_fusion.1, bf16[128,64,128]{2,1,0:T(8,128)(2,1)S(1)} %copy-done.1), kind=kLoop, calls=%fused_computation.35 | loop fusion | flops 6291456 | bytes 4260864 | tf_op jit(solution)/shard_map/convert_element_type | solution.py:39
  23.2 12.3 %all_gather.6 = f32[4,64,512]{2,0,1:T(4,128)} all-gather(f32[4,64,128]{2,0,1:T(4,128)S(1)} %convolution_bitcast_fusion.1), channel_id=1, replica_groups=mesh['row'=4,'col'=8] {'row'}, dimensions={2}, use_global_device_ids=true | all-gather | bytes 655360 | tf_op jit(solution)/shard_map/all_gather | solution.py:122
  35.5 3.8 %all-to-all-start = ((bf16[128,64,128]{2,0,1:T(8,128)(2,1)}), bf16[128,64,128]{2,0,1:T(8,128)(2,1)S(1)}, u32[]{:S(2)}, u32[]{:S(2)}) async-start(bf16[128,64,128]{2,0,1:T(8,128)(2,1)} %copy-done.3), calls=%async_computation | async-start | bytes 4194304 | tf_op jit(solution)/shard_map/all_to_all | solution.py:123
  39.5 23.0 %all-to-all-done = bf16[128,64,128]{2,0,1:T(8,128)(2,1)S(1)} async-done(((bf16[128,64,128]{2,0,1:T(8,128)(2,1)}), bf16[128,64,128]{2,0,1:T(8,128)(2,1)S(1)}, u32[]{:S(2)}, u32[]{:S(2)}) %all-to-all-start) | async-done | bytes 2097184 | tf_op jit(solution)/shard_map/all_to_all | solution.py:123
  63.4 6.3 %fusion.39 = (bf16[512,16,384]{2,0,1:T(8,128)(2,1)S(1)}, f32[512,16,384]{2,0,1:T(8,128)}) fusion(bf16[512,16,128]{2,0,1:T(8,128)(2,1)S(1)} %bitcast.106, bf16[128,512]{1,0:T(8,128)(2,1)S(1)} %copy-done.6), kind=kOutput, calls=%fused_computation.74 | convolution fusion | flops 808452096 | bytes 21069824 | tf_op jit(solution)/shard_map/dot_general | solution.py:125
  69.7 3.2 fusion.38
  72.9 2.9 copy.79
  75.8 2.2 reshape.149
  78.0 2.9 copy.80
  80.9 2.3 reshape.150
  83.2 4.2 %fusion.21 = bf16[512,16,128]{2,0,1:T(8,128)(2,1)} fusion(f32[512,16,384]{2,0,1:T(8,128)} %get-tuple-element.299), kind=kLoop, calls=%fused_computation.38 | loop fusion | flops 2097152 | bytes 6291456 | tf_op jit(solution)/shard_map/convert_element_type | solution.py:131
  87.4 5.4 %copy.101 = f32[4,8,64,512]{3,2,0,1:T(8,128)} copy(f32[4,8,64,512]{3,0,2,1:T(4,128)} %bitcast.108) | data formatting | bytes 8388608 | tf_op jit(solution)/shard_map/reshape | solution.py:141
  92.8 212.3 %while.27 = (s32[]{:T(128)}, bf16[8,64,16,128]{3,2,1,0:T(8,128)(2,1)}, bf16[512,16,128]{0,2,1:T(8,128)(2,1)}, bf16[512,16,128]{0,2,1:T(8,128)(2,1)}, f32[8,4,64,...) while((s32[]{:T(128)}, ...), condition=%wide.wide.region_11.12_spmd, body=%wide.wide.region_3.11_spmd.sunk | while | flops 72364288 | bytes 25006472 | solution.py:151
  95.5 3.4 copy.116
  98.8 3.5 copy.120
  102.4 15.7 %while.28 = (s32[]{:T(128)}, f32[4,16,64]{2,1,0:T(8,128)S(1)}, f32[4,16,64]{2,1,0:T(8,128)S(1)}, f32[64,16,4,32]{0,3,2,1:T(8,128)S(1)}, f32[4,128]{1,0:T(4,128)S...) while((s32[]{:T(128)}, f32[4,16,64]{2,1,0:T(8,128)S(1)}, ...), condition=%wide.region_10.10_spmd, body=%wide.region_4.9_spmd.sunk | while | flops 72102144 | bytes 9457287 | solution.py:103
  103.8 5.2 %conditional.2 = ((f32[4,16,64]{2,1,0:T(8,128)S(1)}, f32[4,16,64]{2,1,0:T(8,128)S(1)}, f32[64,16,4,32]{0,3,2,1:T(8,128)S(1)})) conditional(s32[]{:T(128)} %convert_element_type.93, (f32[4,16,64]{2,1,0:T(8,128)S(1)}, f32[4,16,64]{2,1,0:T(8,128)S(1)}, f32[64,16,4,32]{0,3,2,1:T(8,128)S(1)}) %tuple.72, (f32[1,128]{1,0:T(1,128)S(1)}, ...), branch_computations={%region_6.5_spmd, %region_7.8_spmd} | conditional | flops 72102016 | bytes 9456036 | solution.py:98
  111.6 5.2 %conditional.2 = ((f32[4,16,64]{2,1,0:T(8,128)S(1)}, f32[4,16,64]{2,1,0:T(8,128)S(1)}, f32[64,16,4,32]{0,3,2,1:T(8,128)S(1)})) conditional(s32[]{:T(128)} %convert_element_type.93, (f32[4,16,64]{2,1,0:T(8,128)S(1)}, f32[4,16,64]{2,1,0:T(8,128)S(1)}, f32[64,16,4,32]{0,3,2,1:T(8,128)S(1)}) %tuple.72, (f32[1,128]{1,0:T(1,128)S(1)}, ...), branch_computations={%region_6.5_spmd, %region_7.8_spmd} | conditional | flops 72102016 | bytes 9456036 | solution.py:98
  122.0 3.4 copy.116
  125.4 3.5 copy.120
  129.0 15.7 %while.28 = (s32[]{:T(128)}, f32[4,16,64]{2,1,0:T(8,128)S(1)}, f32[4,16,64]{2,1,0:T(8,128)S(1)}, f32[64,16,4,32]{0,3,2,1:T(8,128)S(1)}, f32[4,128]{1,0:T(4,128)S...) while((s32[]{:T(128)}, f32[4,16,64]{2,1,0:T(8,128)S(1)}, ...), condition=%wide.region_10.10_spmd, body=%wide.region_4.9_spmd.sunk | while | flops 72102144 | bytes 9457287 | solution.py:103
  130.3 5.2 %conditional.2 = ((f32[4,16,64]{2,1,0:T(8,128)S(1)}, f32[4,16,64]{2,1,0:T(8,128)S(1)}, f32[64,16,4,32]{0,3,2,1:T(8,128)S(1)})) conditional(s32[]{:T(128)} %convert_element_type.93, (f32[4,16,64]{2,1,0:T(8,128)S(1)}, f32[4,16,64]{2,1,0:T(8,128)S(1)}, f32[64,16,4,32]{0,3,2,1:T(8,128)S(1)}) %tuple.72, (f32[1,128]{1,0:T(1,128)S(1)}, ...), branch_computations={%region_6.5_spmd, %region_7.8_spmd} | conditional | flops 72102016 | bytes 9456036 | solution.py:98
  130.3 2.0 fusion.1
  138.2 5.2 %conditional.2 = ((f32[4,16,64]{2,1,0:T(8,128)S(1)}, f32[4,16,64]{2,1,0:T(8,128)S(1)}, f32[64,16,4,32]{0,3,2,1:T(8,128)S(1)})) conditional(s32[]{:T(128)} %convert_element_type.93, (f32[4,16,64]{2,1,0:T(8,128)S(1)}, f32[4,16,64]{2,1,0:T(8,128)S(1)}, f32[64,16,4,32]{0,3,2,1:T(8,128)S(1)}) %tuple.72, (f32[1,128]{1,0:T(1,128)S(1)}, ...), branch_computations={%region_6.5_spmd, %region_7.8_spmd} | conditional | flops 72102016 | bytes 9456036 | solution.py:98
  148.5 3.4 copy.116
  151.9 3.5 copy.120
  155.5 15.7 %while.28 = (s32[]{:T(128)}, f32[4,16,64]{2,1,0:T(8,128)S(1)}, f32[4,16,64]{2,1,0:T(8,128)S(1)}, f32[64,16,4,32]{0,3,2,1:T(8,128)S(1)}, f32[4,128]{1,0:T(4,128)S...) while((s32[]{:T(128)}, f32[4,16,64]{2,1,0:T(8,128)S(1)}, ...), condition=%wide.region_10.10_spmd, body=%wide.region_4.9_spmd.sunk | while | flops 72102144 | bytes 9457287 | solution.py:103
  156.8 5.2 %conditional.2 = ((f32[4,16,64]{2,1,0:T(8,128)S(1)}, f32[4,16,64]{2,1,0:T(8,128)S(1)}, f32[64,16,4,32]{0,3,2,1:T(8,128)S(1)})) conditional(s32[]{:T(128)} %convert_element_type.93, (f32[4,16,64]{2,1,0:T(8,128)S(1)}, f32[4,16,64]{2,1,0:T(8,128)S(1)}, f32[64,16,4,32]{0,3,2,1:T(8,128)S(1)}) %tuple.72, (f32[1,128]{1,0:T(1,128)S(1)}, ...), branch_computations={%region_6.5_spmd, %region_7.8_spmd} | conditional | flops 72102016 | bytes 9456036 | solution.py:98
  156.9 2.0 fusion.1
  164.7 5.2 %conditional.2 = ((f32[4,16,64]{2,1,0:T(8,128)S(1)}, f32[4,16,64]{2,1,0:T(8,128)S(1)}, f32[64,16,4,32]{0,3,2,1:T(8,128)S(1)})) conditional(s32[]{:T(128)} %convert_element_type.93, (f32[4,16,64]{2,1,0:T(8,128)S(1)}, f32[4,16,64]{2,1,0:T(8,128)S(1)}, f32[64,16,4,32]{0,3,2,1:T(8,128)S(1)}) %tuple.72, (f32[1,128]{1,0:T(1,128)S(1)}, ...), branch_computations={%region_6.5_spmd, %region_7.8_spmd} | conditional | flops 72102016 | bytes 9456036 | solution.py:98
  175.1 3.4 copy.116
  178.4 3.5 copy.120
  182.1 15.7 %while.28 = (s32[]{:T(128)}, f32[4,16,64]{2,1,0:T(8,128)S(1)}, f32[4,16,64]{2,1,0:T(8,128)S(1)}, f32[64,16,4,32]{0,3,2,1:T(8,128)S(1)}, f32[4,128]{1,0:T(4,128)S...) while((s32[]{:T(128)}, f32[4,16,64]{2,1,0:T(8,128)S(1)}, ...), condition=%wide.region_10.10_spmd, body=%wide.region_4.9_spmd.sunk | while | flops 72102144 | bytes 9457287 | solution.py:103
  183.4 5.2 %conditional.2 = ((f32[4,16,64]{2,1,0:T(8,128)S(1)}, f32[4,16,64]{2,1,0:T(8,128)S(1)}, f32[64,16,4,32]{0,3,2,1:T(8,128)S(1)})) conditional(s32[]{:T(128)} %convert_element_type.93, (f32[4,16,64]{2,1,0:T(8,128)S(1)}, f32[4,16,64]{2,1,0:T(8,128)S(1)}, f32[64,16,4,32]{0,3,2,1:T(8,128)S(1)}) %tuple.72, (f32[1,128]{1,0:T(1,128)S(1)}, ...), branch_computations={%region_6.5_spmd, %region_7.8_spmd} | conditional | flops 72102016 | bytes 9456036 | solution.py:98
  191.2 5.2 %conditional.2 = ((f32[4,16,64]{2,1,0:T(8,128)S(1)}, f32[4,16,64]{2,1,0:T(8,128)S(1)}, f32[64,16,4,32]{0,3,2,1:T(8,128)S(1)})) conditional(s32[]{:T(128)} %convert_element_type.93, (f32[4,16,64]{2,1,0:T(8,128)S(1)}, f32[4,16,64]{2,1,0:T(8,128)S(1)}, f32[64,16,4,32]{0,3,2,1:T(8,128)S(1)}) %tuple.72, (f32[1,128]{1,0:T(1,128)S(1)}, ...), branch_computations={%region_6.5_spmd, %region_7.8_spmd} | conditional | flops 72102016 | bytes 9456036 | solution.py:98
  201.6 3.4 copy.116
  205.0 3.5 copy.120
  208.6 15.7 %while.28 = (s32[]{:T(128)}, f32[4,16,64]{2,1,0:T(8,128)S(1)}, f32[4,16,64]{2,1,0:T(8,128)S(1)}, f32[64,16,4,32]{0,3,2,1:T(8,128)S(1)}, f32[4,128]{1,0:T(4,128)S...) while((s32[]{:T(128)}, f32[4,16,64]{2,1,0:T(8,128)S(1)}, ...), condition=%wide.region_10.10_spmd, body=%wide.region_4.9_spmd.sunk | while | flops 72102144 | bytes 9457287 | solution.py:103
  209.9 5.2 %conditional.2 = ((f32[4,16,64]{2,1,0:T(8,128)S(1)}, f32[4,16,64]{2,1,0:T(8,128)S(1)}, f32[64,16,4,32]{0,3,2,1:T(8,128)S(1)})) conditional(s32[]{:T(128)} %convert_element_type.93, (f32[4,16,64]{2,1,0:T(8,128)S(1)}, f32[4,16,64]{2,1,0:T(8,128)S(1)}, f32[64,16,4,32]{0,3,2,1:T(8,128)S(1)}) %tuple.72, (f32[1,128]{1,0:T(1,128)S(1)}, ...), branch_computations={%region_6.5_spmd, %region_7.8_spmd} | conditional | flops 72102016 | bytes 9456036 | solution.py:98
  217.8 5.2 %conditional.2 = ((f32[4,16,64]{2,1,0:T(8,128)S(1)}, f32[4,16,64]{2,1,0:T(8,128)S(1)}, f32[64,16,4,32]{0,3,2,1:T(8,128)S(1)})) conditional(s32[]{:T(128)} %convert_element_type.93, (f32[4,16,64]{2,1,0:T(8,128)S(1)}, f32[4,16,64]{2,1,0:T(8,128)S(1)}, f32[64,16,4,32]{0,3,2,1:T(8,128)S(1)}) %tuple.72, (f32[1,128]{1,0:T(1,128)S(1)}, ...), branch_computations={%region_6.5_spmd, %region_7.8_spmd} | conditional | flops 72102016 | bytes 9456036 | solution.py:98
  228.2 3.4 copy.116
  231.5 3.5 copy.120
  235.1 15.7 %while.28 = (s32[]{:T(128)}, f32[4,16,64]{2,1,0:T(8,128)S(1)}, f32[4,16,64]{2,1,0:T(8,128)S(1)}, f32[64,16,4,32]{0,3,2,1:T(8,128)S(1)}, f32[4,128]{1,0:T(4,128)S...) while((s32[]{:T(128)}, f32[4,16,64]{2,1,0:T(8,128)S(1)}, ...), condition=%wide.region_10.10_spmd, body=%wide.region_4.9_spmd.sunk | while | flops 72102144 | bytes 9457287 | solution.py:103
  236.5 5.2 %conditional.2 = ((f32[4,16,64]{2,1,0:T(8,128)S(1)}, f32[4,16,64]{2,1,0:T(8,128)S(1)}, f32[64,16,4,32]{0,3,2,1:T(8,128)S(1)})) conditional(s32[]{:T(128)} %convert_element_type.93, (f32[4,16,64]{2,1,0:T(8,128)S(1)}, f32[4,16,64]{2,1,0:T(8,128)S(1)}, f32[64,16,4,32]{0,3,2,1:T(8,128)S(1)}) %tuple.72, (f32[1,128]{1,0:T(1,128)S(1)}, ...), branch_computations={%region_6.5_spmd, %region_7.8_spmd} | conditional | flops 72102016 | bytes 9456036 | solution.py:98
  244.3 5.2 %conditional.2 = ((f32[4,16,64]{2,1,0:T(8,128)S(1)}, f32[4,16,64]{2,1,0:T(8,128)S(1)}, f32[64,16,4,32]{0,3,2,1:T(8,128)S(1)})) conditional(s32[]{:T(128)} %convert_element_type.93, (f32[4,16,64]{2,1,0:T(8,128)S(1)}, f32[4,16,64]{2,1,0:T(8,128)S(1)}, f32[64,16,4,32]{0,3,2,1:T(8,128)S(1)}) %tuple.72, (f32[1,128]{1,0:T(1,128)S(1)}, ...), branch_computations={%region_6.5_spmd, %region_7.8_spmd} | conditional | flops 72102016 | bytes 9456036 | solution.py:98
  254.7 3.4 copy.116
  258.1 3.5 copy.120
  261.7 15.7 %while.28 = (s32[]{:T(128)}, f32[4,16,64]{2,1,0:T(8,128)S(1)}, f32[4,16,64]{2,1,0:T(8,128)S(1)}, f32[64,16,4,32]{0,3,2,1:T(8,128)S(1)}, f32[4,128]{1,0:T(4,128)S...) while((s32[]{:T(128)}, f32[4,16,64]{2,1,0:T(8,128)S(1)}, ...), condition=%wide.region_10.10_spmd, body=%wide.region_4.9_spmd.sunk | while | flops 72102144 | bytes 9457287 | solution.py:103
  263.0 5.2 %conditional.2 = ((f32[4,16,64]{2,1,0:T(8,128)S(1)}, f32[4,16,64]{2,1,0:T(8,128)S(1)}, f32[64,16,4,32]{0,3,2,1:T(8,128)S(1)})) conditional(s32[]{:T(128)} %convert_element_type.93, (f32[4,16,64]{2,1,0:T(8,128)S(1)}, f32[4,16,64]{2,1,0:T(8,128)S(1)}, f32[64,16,4,32]{0,3,2,1:T(8,128)S(1)}) %tuple.72, (f32[1,128]{1,0:T(1,128)S(1)}, ...), branch_computations={%region_6.5_spmd, %region_7.8_spmd} | conditional | flops 72102016 | bytes 9456036 | solution.py:98
  270.9 5.2 %conditional.2 = ((f32[4,16,64]{2,1,0:T(8,128)S(1)}, f32[4,16,64]{2,1,0:T(8,128)S(1)}, f32[64,16,4,32]{0,3,2,1:T(8,128)S(1)})) conditional(s32[]{:T(128)} %convert_element_type.93, (f32[4,16,64]{2,1,0:T(8,128)S(1)}, f32[4,16,64]{2,1,0:T(8,128)S(1)}, f32[64,16,4,32]{0,3,2,1:T(8,128)S(1)}) %tuple.72, (f32[1,128]{1,0:T(1,128)S(1)}, ...), branch_computations={%region_6.5_spmd, %region_7.8_spmd} | conditional | flops 72102016 | bytes 9456036 | solution.py:98
  281.3 3.4 copy.116
  284.6 3.5 copy.120
  288.2 15.7 %while.28 = (s32[]{:T(128)}, f32[4,16,64]{2,1,0:T(8,128)S(1)}, f32[4,16,64]{2,1,0:T(8,128)S(1)}, f32[64,16,4,32]{0,3,2,1:T(8,128)S(1)}, f32[4,128]{1,0:T(4,128)S...) while((s32[]{:T(128)}, f32[4,16,64]{2,1,0:T(8,128)S(1)}, ...), condition=%wide.region_10.10_spmd, body=%wide.region_4.9_spmd.sunk | while | flops 72102144 | bytes 9457287 | solution.py:103
  289.5 5.2 %conditional.2 = ((f32[4,16,64]{2,1,0:T(8,128)S(1)}, f32[4,16,64]{2,1,0:T(8,128)S(1)}, f32[64,16,4,32]{0,3,2,1:T(8,128)S(1)})) conditional(s32[]{:T(128)} %convert_element_type.93, (f32[4,16,64]{2,1,0:T(8,128)S(1)}, f32[4,16,64]{2,1,0:T(8,128)S(1)}, f32[64,16,4,32]{0,3,2,1:T(8,128)S(1)}) %tuple.72, (f32[1,128]{1,0:T(1,128)S(1)}, ...), branch_computations={%region_6.5_spmd, %region_7.8_spmd} | conditional | flops 72102016 | bytes 9456036 | solution.py:98
  297.4 5.2 %conditional.2 = ((f32[4,16,64]{2,1,0:T(8,128)S(1)}, f32[4,16,64]{2,1,0:T(8,128)S(1)}, f32[64,16,4,32]{0,3,2,1:T(8,128)S(1)})) conditional(s32[]{:T(128)} %convert_element_type.93, (f32[4,16,64]{2,1,0:T(8,128)S(1)}, f32[4,16,64]{2,1,0:T(8,128)S(1)}, f32[64,16,4,32]{0,3,2,1:T(8,128)S(1)}) %tuple.72, (f32[1,128]{1,0:T(1,128)S(1)}, ...), branch_computations={%region_6.5_spmd, %region_7.8_spmd} | conditional | flops 72102016 | bytes 9456036 | solution.py:98
  310.8 11.1 %collective-permute-done = bf16[128,16,128]{2,1,0:T(8,128)(2,1)S(1)} collective-permute-done((bf16[128,16,128]{2,1,0:T(8,128)(2,1)S(1)}, bf16[128,16,128]{2,1,0:T(8,128)(2,1)S(1)}, u32[]{:S(2)}, u32[]{:S(2)}) %collective-permute-start) | collective-permute-done | bytes 524320 | tf_op jit(solution)/shard_map/ppermute | solution.py:30
  321.9 9.5 %collective-permute-done.1 = bf16[128,16,128]{2,1,0:T(8,128)(2,1)S(1)} collective-permute-done((bf16[128,16,128]{2,1,0:T(8,128)(2,1)S(1)}, bf16[128,16,128]{2,1,0:T(8,128)(2,1)S(1)}, u32[]{:S(2)}, u32[]{:S(2)}) %collective-permute-start.1) | collective-permute-done | bytes 524320 | tf_op jit(solution)/shard_map/ppermute | solution.py:30
  331.4 2.6 pad_maximum_fusion
  334.0 2.5 gather_fusion
  337.0 2.6 copy.83
  339.6 8.7 %fusion.20 = bf16[128,64,128]{2,0,1:T(8,128)(2,1)} fusion(f32[128,64]{0,1:T(8,128)S(1)} %broadcast_multiply_fusion, f32[128]{0:T(128)S(1)} %copy-done.11, bf16[128,64,128]{2,1,0:T(8,128)(2,1)S(1)} %copy-done.2, f32[128,64,128]{2,1,0:T(8,128)} %bitcast.109, bf16[128,64,128]{2,0,1:T(8,128)(2,1)} %copy-done.3, f32[128]{0:T(128)S(1)} %copy-done.12, ...), kind=kOutput, calls=%fused_computation.36 | convolution fusion | flops 548405248 | bytes 10585088 | tf_op jit(solution)/shard_map/dot_general | solution.py:158
  348.3 4.3 %copy.85 = bf16[128,64,128]{2,1,0:T(8,128)(2,1)} copy(bf16[128,64,128]{2,0,1:T(8,128)(2,1)} %fusion.20) | data formatting | bytes 4194304 | tf_op jit(solution)/shard_map/convert_element_type | solution.py:165
  (342 shorter events, 139.7 us)
Async XLA Ops:
  6.5 333.1 %copy-start = (bf16[128,128]{1,0:T(8,128)(2,1)S(1)}, bf16[128,128]{1,0:T(8,128)(2,1)}, u32[]{:S(2)}) copy-start(bf16[128,128]{1,0:T(8,128)(2,1)} %param.21) | copy-start | bytes 98308
  6.5 3.6 copy-start.1
  6.5 9.7 %copy-start.9 = (f32[128]{0:T(128)S(1)}, f32[128]{0:T(128)}, u32[]{:S(2)}) copy-start(f32[128]{0:T(128)} %param.16) | copy-start | bytes 1540
  6.5 9.7 %copy-start.8 = (f32[128]{0:T(128)S(1)}, f32[128]{0:T(128)}, u32[]{:S(2)}) copy-start(f32[128]{0:T(128)} %param.17) | copy-start | bytes 1540
  6.5 80.9 %all-gather.2.cloned.1.call-start = ((), (), s32[]{:S(2)}) async-start(), calls=%async_computation.1 | async-start | bytes 4718592 | tf_op jit(solution)/shard_map/all_gather | solution.py:134
  16.3 6.3 %copy-start.7 = (bf16[128,4]{0,1:T(4,128)(2,1)S(1)}, bf16[128,4]{0,1:T(4,128)(2,1)}, u32[]{:S(2)}) copy-start(bf16[128,4]{0,1:T(4,128)(2,1)} %param.20) | copy-start | bytes 3076
  21.2 1.3 copy-start.3
  35.5 3.8 %copy-start.10 = (s32[4]{0:T(128)S(1)}, s32[4]{0:T(128)}, u32[]{:S(2)}) copy-start(s32[4]{0:T(128)} %param.23) | copy-start | bytes 52
  35.5 27.0 %all-to-all-start = ((bf16[128,64,128]{2,0,1:T(8,128)(2,1)}), bf16[128,64,128]{2,0,1:T(8,128)(2,1)S(1)}, u32[]{:S(2)}, u32[]{:S(2)}) async-start(bf16[128,64,128]{2,0,1:T(8,128)(2,1)} %copy-done.3), calls=%async_computation | async-start | bytes 4194304 | tf_op jit(solution)/shard_map/all_to_all | solution.py:123
  62.5 0.9 copy-start.6
  75.8 2.2 copy-start.4
  80.9 2.3 copy-start.5
  307.0 14.9 %collective-permute-start = (bf16[128,16,128]{2,1,0:T(8,128)(2,1)S(1)}, bf16[128,16,128]{2,1,0:T(8,128)(2,1)S(1)}, u32[]{:S(2)}, u32[]{:S(2)}) collective-permute-start(bf16[128,16,128]{2,1,0:T(8,128)(2,1)S(1)} %get-tuple-element.297), channel_id=1, source_target_pairs={{0,8},{8,0},{16,24},{24,16},{1,9},{9,1},{17,25},{25,17},{2,10},{10... | collective-permute-start | bytes 1572872 | tf_op jit(solution)/shard_map/ppermute | solution.py:30
  308.5 22.9 %collective-permute-start.1 = (bf16[128,16,128]{2,1,0:T(8,128)(2,1)S(1)}, bf16[128,16,128]{2,1,0:T(8,128)(2,1)S(1)}, u32[]{:S(2)}, u32[]{:S(2)}) collective-permute-start(bf16[128,16,128]{2,1,0:T(8,128)(2,1)S(1)} %get-tuple-element.296), channel_id=1, source_target_pairs={{0,16},{8,24},{16,0},{24,8},{1,17},{9,25},{17,1},{25,9},{2,18},{10... | collective-permute-start | bytes 1572872 | tf_op jit(solution)/shard_map/ppermute | solution.py:30
  309.0 22.4 %collective-permute-start.2 = (bf16[128,16,128]{2,1,0:T(8,128)(2,1)S(1)}, bf16[128,16,128]{2,1,0:T(8,128)(2,1)}, u32[]{:S(2)}, u32[]{:S(2)}) collective-permute-start(bf16[128,16,128]{2,1,0:T(8,128)(2,1)S(1)} %get-tuple-element.295), channel_id=1, source_target_pairs={{0,24},{8,16},{16,8},{24,0},{1,25},{9,17},{17,9},{25,1},{2,26},{10... | collective-permute-start | bytes 1572872 | tf_op jit(solution)/shard_map/ppermute | solution.py:30
  337.0 2.6 copy-start.2
  337.0 2.6 copy-start.11
  337.0 2.6 copy-start.12
Sparse Core Ops, SparseCore 0:
  35.6 47.1 all-gather.1
